TPU v7x, 128 devices: a whole 4x4x4 slice. The times are simulated.
128 devices in a mesh: dp: 64 (over y, z_lo, x, core), rep: 2 (over z_hi).
Axes of the slice: x: 4, y: 4, z: 4 (z_hi: 2, z_lo: 2; z = z_hi * 2 + z_lo), core: 2. Of those that a mesh axis runs over, the one named last changes fastest.
Arguments:
- queries: bfloat16 [8192, 2048], P(('dp', 'rep')), may hold values from -24 to 24
- documents: bfloat16 [8192, 2048], P(('dp', 'rep')), may hold values from -24 to 24
- partner: int32 [8192], P(('dp', 'rep')), may hold values from 0 to 8191, each once
Outputs:
- grad_queries: float32 [8192, 2048], P(('dp', 'rep'))
- grad_documents: float32 [8192, 2048], P(('dp', 'rep'))
Inputs may be any that keep to these rules, and one draw needn't show every extreme that they name: `partner`: every document index appears exactly once.
All inputs are finite; a program needn't handle non-finite values.
Results may differ from a plain program's by a relative error of at most 0.0031.
Values may be sent and summed in bfloat16 or wider, within the bound.
A program may use at most 256 MiB of HBM per device.

v0:
```python
import jax
import jax.numpy as jnp
from jax import lax
from jax.sharding import Mesh
from jax.sharding import PartitionSpec as P

WIDTHS = 9
DP = ("dp_0", "dp_1", "dp_2", "dp_3")
DP_REP = ("dp_0", "dp_1", "dp_2", "dp_3", "rep")
logit_gain = 3.0


def contract(first_op, second_op):
    return lax.dot_general(
        first_op, second_op, (((1,), (1,)), ((), ())), preferred_element_type=jnp.float32
    )


def width_list(feature_dim):
    return [feature_dim >> WIDTHS - 1 - nested for nested in range(WIDTHS)]


def scores(first_op, second_op):
    uppers = width_list(first_op.shape[1])
    result = []
    running = jnp.zeros((first_op.shape[0], second_op.shape[0]), jnp.float32)
    lower_col = 0
    for upper_col in uppers:
        running = running + contract(
            first_op[:, lower_col:upper_col], second_op[:, lower_col:upper_col]
        )
        result.append(running * (logit_gain * upper_col ** (-0.5)))
        lower_col = upper_col
    return result


def band_sums(logit_list, total_list, target, uppers):
    bands = [None] * len(uppers)
    running = None
    for nested in reversed(range(len(uppers))):
        scale = logit_gain * uppers[nested] ** (-0.5)
        weight = (jnp.exp(logit_list[nested] - total_list[nested]) - target) * scale
        running = weight if running is None else running + weight
        bands[nested] = running.astype(jnp.bfloat16)
    return bands


def spread(bands, operand, uppers, transposed):
    pieces = []
    lower_col = 0
    for nested, upper_col in enumerate(uppers):
        block_part = operand[:, lower_col:upper_col]
        if transposed:
            product = lax.dot_general(
                bands[nested],
                block_part,
                (((0,), (0,)), ((), ())),
                preferred_element_type=jnp.float32,
            )
        else:
            product = jnp.dot(bands[nested], block_part, preferred_element_type=jnp.float32)
        pieces.append(product)
        lower_col = upper_col
    return jnp.concatenate(pieces, axis=1)


Q_AXES = ("dp_0", "dp_1")
D_AXES = ("dp_2", "dp_3", "rep")


def on_device(queries, documents, partner):
    own_rows = queries.shape[0]
    uppers = width_list(queries.shape[1])
    rows = lax.all_gather(queries, Q_AXES, axis=0, tiled=True)
    row_partner = lax.all_gather(partner, Q_AXES, axis=0, tiled=True)
    docs = lax.all_gather(documents, D_AXES, axis=0, tiled=True)
    x_size, core_size, rep_size = [lax.axis_size(name) for name in D_AXES]
    block = lax.axis_index(Q_AXES)
    shards = block * (x_size * core_size * rep_size)
    col_ids = shards * own_rows + jnp.arange(docs.shape[0], dtype=jnp.int32)
    target = (row_partner[:, None] == col_ids[None, :]).astype(jnp.float32)
    logit_list = scores(rows, docs)
    row_peaks = jnp.stack([jnp.max(logits, axis=1) for logits in logit_list])
    masses = jnp.stack(
        [
            jnp.sum(jnp.exp(logits - row_peaks[nested][:, None]), axis=1)
            for nested, logits in enumerate(logit_list)
        ]
    )
    parts = lax.all_gather(row_peaks + jnp.log(masses), Q_AXES, axis=0)
    peak = jnp.max(parts, axis=0)
    totals = peak + jnp.log(jnp.sum(jnp.exp(parts - peak[None]), axis=0))
    bands = band_sums(
        logit_list, [totals[nested][:, None] for nested in range(len(uppers))], target, uppers
    )
    grad_documents = lax.psum_scatter(
        spread(bands, rows, uppers, True), D_AXES, scatter_dimension=0, tiled=True
    )
    grad_queries = lax.psum_scatter(
        spread(bands, docs, uppers, False), Q_AXES, scatter_dimension=0, tiled=True
    )
    return (grad_queries, grad_documents)


def solution(mesh):
    finer = Mesh(
        mesh.devices.reshape(4, 2, 4, 2, mesh.shape["rep"]), ("dp_0", "dp_1", "dp_2", "dp_3", "rep")
    )
    placed = (P(DP_REP, None), P(DP_REP, None), P(DP_REP))
    return jax.shard_map(
        on_device,
        mesh=finer,
        in_specs=placed,
        out_specs=(P(DP_REP, None), P(DP_REP, None)),
        check_vma=False,
    )
```

profile of v0, /device:TPU:0, one launch (start us, length us, event | category | flops | bytes accessed | tf_op | source)
XLA Modules:
  0.0 406.1 jit_solution(15997544416432338773)
XLA Ops:
  8.7 1.2 dynamic-slice
  11.5 12.0 %all-reduce = s32[512]{0:T(512)S(1)} all-reduce(s32[512]{0:T(512)S(1)} %dynamic-update-slice), channel_id=1, replica_groups=mesh['dp_0'=4,'dp_1'=2,'dp_2'=4,'dp_3'=2,'rep'=2] {'dp_0','dp_1'}, use_global_device_ids=true, to_apply=%add | all-reduce | flops 512 | bytes 4096
  23.5 39.8 %all-gather.3.cloned.1.call-done = bf16[512,2048]{1,0:T(8,128)(2,1)} async-done(((bf16[64,2048]{1,0:T(8,128)(2,1)}), bf16[512,2048]{1,0:T(8,128)(2,1)}) %all-gather.3.cloned.1.call-update) | async-done | bytes 2097168 | tf_op jit(solution)/shard_map/all_gather | solution.py:74
  63.3 59.5 %all-gather.5.cloned.1.call-done = bf16[1024,2048]{1,0:T(8,128)(2,1)} async-done(((bf16[64,2048]{1,0:T(8,128)(2,1)}), bf16[1024,2048]{1,0:T(8,128)(2,1)}) %all-gather.5.cloned.1.call-update) | async-done | bytes 4194320 | tf_op jit(solution)/shard_map/all_gather | solution.py:76
  122.8 1.5 multiply_reduce_fusion.7
  124.8 1.6 multiply_reduce_fusion.6
  127.0 1.8 multiply_reduce_fusion.5
  129.3 1.8 multiply_reduce_fusion.4
  131.7 1.8 multiply_reduce_fusion.3
  134.1 1.7 multiply_reduce_fusion.2
  136.3 1.9 multiply_reduce_fusion.1
  138.7 2.4 multiply_reduce_fusion
  141.7 3.5 fusion.92
  145.2 1.4 copy-done.16
  147.2 28.6 %all_gather.15 = f32[8,9,512]{2,1,0:T(8,128)S(1)} all-gather(f32[1,9,512]{2,1,0:T(8,128)S(1)} %log_add_fusion.1), channel_id=1, replica_groups=mesh['dp_0'=4,'dp_1'=2,'dp_2'=4,'dp_3'=2,'rep'=2] {'dp_0','dp_1'}, dimensions={0}, use_global_device_ids=true | all-gather | bytes 165888 | tf_op jit(solution)/shard_map/all_gather | solution.py:90
  176.0 9.6 %fusion.17 = (bf16[512,1024]{1,0:T(8,128)(2,1)S(1)}, bf16[512,1024]{1,0:T(8,128)(2,1)S(1)}, bf16[512,1024]{1,0:T(8,128)(2,1)S(1)}, bf16[512,1024]{1,0:T(8,128)(2...) fusion(f32[512,1024]{1,0:T(8,128)S(1)} %get-tuple-element.24, ...), kind=kLoop, calls=%fused_computation.27 | loop fusion | flops 27787264 | bytes 27287552 | tf_op jit(solution)/shard_map/convert_element_type | solution.py:44
  185.8 1.4 fusion.18
  187.6 1.2 fusion.48
  188.9 1.2 fusion.45
  190.1 1.2 fusion.42
  193.7 1.2 fusion.33
  195.0 1.7 fusion.27
  196.7 5.9 %concatenate.20 = f32[512,2048]{1,0:T(8,128)} concatenate(f32[512,8]{1,0:T(8,128)S(1)} %fusion.66, f32[512,8]{1,0:T(8,128)} %fusion.48, f32[512,16]{1,0:T(8,128)} %fusion.45, f32[512,32]{1,0:T(8,128)} %fusion.42, f32[512,64]{1,0:T(8,128)} %fusion.39, f32[512,128]{1,0:T(8,128)} %fusion.36, f32[512,256]{1,0:T(8,128)} %fusion.33, f32[512,512]{1,0:T(8,128)} %fusion.27, ...), dimensions={1} | concatenate | bytes 8388608 | tf_op jit(solution)/shard_map/concatenate | solution.py:64
  202.7 2.3 convolution_dynamic-update-slice_fusion.8
  205.0 2.0 convolution_dynamic-update-slice_fusion.7
  206.9 2.0 convolution_dynamic-update-slice_fusion.6
  212.2 1.5 convolution_dynamic-update-slice_fusion.2
  213.8 2.1 convolution_dynamic-update-slice_fusion.1
  215.8 3.5 convolution_dynamic-update-slice_fusion
  219.4 9.1 %copy.31 = f32[1024,2048]{1,0:T(8,128)} copy(f32[1024,2048]{0,1:T(8,128)} %convolution_dynamic-update-slice_fusion) | data formatting | bytes 16777216
  228.5 62.8 %reduce-scatter.5.cloned.1.call-done = f32[64,2048]{1,0:T(8,128)} async-done(((f32[512,2048]{1,0:T(8,128)}), f32[64,2048]{1,0:T(8,128)}) %reduce-scatter.5.cloned.1.call-update) | async-done | bytes 524304 | tf_op jit(solution)/shard_map/reduce_scatter | solution.py:99
  291.4 108.2 %reduce-scatter.7.cloned.1.call-done = f32[64,2048]{1,0:T(8,128)} async-done(((f32[1024,2048]{1,0:T(8,128)}), f32[64,2048]{1,0:T(8,128)}) %reduce-scatter.7.cloned.1.call-update) | async-done | bytes 524304
  (82 shorter events, 13.6 us)
Async XLA Ops:
  7.2 56.1 %all-gather.3.cloned.1.call-start = ((), (), s32[]{:S(2)}) async-start(), calls=%async_computation.2 | async-start | bytes 2359296 | tf_op jit(solution)/shard_map/all_gather | solution.py:74
  7.9 114.9 %all-gather.5.cloned.1.call-start = ((), (), s32[]{:S(2)}) async-start(), calls=%async_computation.3 | async-start | bytes 4456448 | tf_op jit(solution)/shard_map/all_gather | solution.py:76
  8.6 282.7 %reduce-scatter.5.cloned.1.call-start = ((), (), s32[]{:S(2)}) async-start(), calls=%async_computation.4 | async-start | bytes 4718592 | tf_op jit(solution)/shard_map/reduce_scatter | solution.py:99
  126.5 2.4 copy-start
  128.8 2.3 copy-start.1
  131.2 2.4 copy-start.2
  133.5 2.3 copy-start.3
  135.8 2.4 copy-start.4
  138.2 3.0 copy-start.5
  141.2 4.0 copy-start.6
  145.2 1.4 copy-start.16
  176.0 9.7 %copy-start.17 = (f32[512,1024]{1,0:T(8,128)S(1)}, f32[512,1024]{1,0:T(8,128)}, u32[]{:S(2)}) copy-start(f32[512,1024]{1,0:T(8,128)} %copy-done.16) | copy-start | bytes 6291460
  176.0 9.7 %copy-start.19 = (bf16[1024,2048]{1,0:T(8,128)(2,1)S(1)}, bf16[1024,2048]{1,0:T(8,128)(2,1)}, u32[]{:S(2)}) copy-start(bf16[1024,2048]{1,0:T(8,128)(2,1)} %all-gather.5.cloned.1.call-done) | copy-start | bytes 12582916
  185.7 1.5 copy-start.15
  185.7 1.9 copy-start.13
  185.7 3.2 copy-start.11
  185.7 5.6 %copy-start.9 = (bf16[512,1024]{1,0:T(8,128)(2,1)}, bf16[512,1024]{1,0:T(8,128)(2,1)S(1)}, u32[]{:S(2)}) copy-start(bf16[512,1024]{1,0:T(8,128)(2,1)S(1)} %get-tuple-element.10) | copy-start | bytes 3145732
  185.7 6.8 %copy-start.7 = (bf16[512,1024]{1,0:T(8,128)(2,1)}, bf16[512,1024]{1,0:T(8,128)(2,1)S(1)}, u32[]{:S(2)}) copy-start(bf16[512,1024]{1,0:T(8,128)(2,1)S(1)} %get-tuple-element.11) | copy-start | bytes 3145732
  185.7 8.0 %copy-start.23 = (bf16[512,1024]{1,0:T(8,128)(2,1)}, bf16[512,1024]{1,0:T(8,128)(2,1)S(1)}, u32[]{:S(2)}) copy-start(bf16[512,1024]{1,0:T(8,128)(2,1)S(1)} %get-tuple-element.12) | copy-start | bytes 3145732
  185.7 9.2 %copy-start.21 = (bf16[512,1024]{1,0:T(8,128)(2,1)}, bf16[512,1024]{1,0:T(8,128)(2,1)S(1)}, u32[]{:S(2)}) copy-start(bf16[512,1024]{1,0:T(8,128)(2,1)S(1)} %get-tuple-element.13) | copy-start | bytes 3145732
  202.6 2.4 copy-start.14
  202.6 4.3 %copy-start.12 = (bf16[512,1024]{1,0:T(8,128)(2,1)S(1)}, bf16[512,1024]{1,0:T(8,128)(2,1)}, u32[]{:S(2)}) copy-start(bf16[512,1024]{1,0:T(8,128)(2,1)} %copy-done.11) | copy-start | bytes 3145732
  202.6 197.0 %reduce-scatter.7.cloned.1.call-start = ((), (), s32[]{:S(2)}) async-start(), calls=%async_computation.5 | async-start | bytes 8912896
  202.7 6.2 %copy-start.20 = (bf16[512,2048]{1,0:T(8,128)(2,1)S(1)}, bf16[512,2048]{1,0:T(8,128)(2,1)}, u32[]{:S(2)}) copy-start(bf16[512,2048]{1,0:T(8,128)(2,1)} %all-gather.3.cloned.1.call-done) | copy-start | bytes 6291460
  205.0 5.0 %copy-start.10 = (bf16[512,1024]{1,0:T(8,128)(2,1)S(1)}, bf16[512,1024]{1,0:T(8,128)(2,1)}, u32[]{:S(2)}) copy-start(bf16[512,1024]{1,0:T(8,128)(2,1)} %copy-done.9) | copy-start | bytes 3145732
  206.9 4.1 %copy-start.8 = (bf16[512,1024]{1,0:T(8,128)(2,1)S(1)}, bf16[512,1024]{1,0:T(8,128)(2,1)}, u32[]{:S(2)}) copy-start(bf16[512,1024]{1,0:T(8,128)(2,1)} %copy-done.7) | copy-start | bytes 3145732
  208.9 3.3 copy-start.24
  211.0 2.7 copy-start.22
  213.8 2.1 copy-start.18
Sparse Core Ops, SparseCore 0:
  9.6 53.6 all-gather.2
  65.7 57.0 all-gather.4
  202.7 88.5 reduce-scatter.4
  296.1 103.3 reduce-scatter.6
where the time goes:
time: 407 us; the launch traced here: 406 us
  waiting for transfers between devices  272 us (67%)
  matrix products  45.7 us (11%)
  blocking collectives  40.7 us (10%)
  local copies, waits for them, and re-layouts  18.8 us (5%)
  between operations  14.7 us (4%)
  other arithmetic  14.4 us (4%)
    unnamed x5, waiting for transfers between devices  110 us
    reduce_scatter x1, waiting for transfers between devices, on_device(): lax.psum_scatter(spread(bands, docs, uppers, False), Q_AXES, scatter_dime...  62.8 us
    all_gather x1, waiting for transfers between devices, on_device(): docs = lax.all_gather(documents, D_AXES, axis=0, tiled=True)  59.5 us
    all_gather x1, waiting for transfers between devices, on_device(): rows = lax.all_gather(queries, Q_AXES, axis=0, tiled=True)  39.8 us
    all_gather x1, blocking collectives, on_device(): parts = lax.all_gather(row_peaks + jnp.log(masses), Q_AXES, axis=0)  28.6 us
    dot_general x9, matrix products, contract(): lax.dot_general(first_op, second_op, (((1,), (1,)), ((), ())), preferred_...  18.1 us
    dot_general x9, matrix products, spread(): lax.dot_general(bands[nested], block_part, (((0,), (0,)), ((), ())), pref...  16.7 us
    unnamed x54, local copies, waits for them, and re-layouts  12.7 us
  transfers between devices with their start and end apart: 4, of which 4 were waited for; matrix products, arithmetic and copies ran while one was open for 7% of the time, Pallas kernels for 0%

commit v1 on v0

--- a/solution.py
+++ b/solution.py
@@ -71,7 +71,10 @@
 def on_device(queries, documents, partner):
     own_rows = queries.shape[0]
     uppers = width_list(queries.shape[1])
-    rows = lax.all_gather(queries, Q_AXES, axis=0, tiled=True)
+    n_dev = lax.axis_size(Q_AXES)
+    blocks = jnp.stack([queries for _ in range(n_dev)])
+    blocks = lax.all_to_all(blocks, Q_AXES, split_axis=0, concat_axis=0)
+    rows = jnp.concatenate(blocks, axis=0)
     row_partner = lax.all_gather(partner, Q_AXES, axis=0, tiled=True)
     docs = lax.all_gather(documents, D_AXES, axis=0, tiled=True)
     x_size, core_size, rep_size = [lax.axis_size(name) for name in D_AXES]

time: 407 us -> 367 us (0.902)
  waiting for transfers between devices: 272 us -> 202 us
  blocking collectives: 40.7 us -> 62.1 us
  starting transfers between devices: 0.16 us -> 6.18 us
    all_gather x1 -> x0, waiting for transfers between devices: 39.8 us -> none  [on_device(): rows = lax.all_gather(queries, Q_AXES, axis=0, tiled=True)]
    all_gather x1, waiting for transfers between devices: 59.5 us -> 30.7 us  [on_device(): docs = lax.all_gather(documents, D_AXES, axis=0, tiled=True)]
    unnamed x1, blocking collectives: 12 us -> 33.5 us
    all_to_all x0 -> x1, starting transfers between devices: none -> 6.07 us  [on_device(): blocks = lax.all_to_all(blocks, Q_AXES, split_axis=0, concat_axis=0)]
    unnamed x5 -> x4, waiting for transfers between devices: 110 us -> 109 us
    unnamed x54 -> x58, local copies, waits for them, and re-layouts: 12.7 us -> 13 us
  transfers between devices with their start and end apart: 4 -> 4, of which waited for: 4 -> 3; matrix products, arithmetic and copies ran while one was open for 7% -> 8% of each run, Pallas kernels for 0% -> 0%
where the time goes in v1:
time: 367 us; the launch traced here: 366 us
  waiting for transfers between devices  202 us (55%)
  blocking collectives  62.1 us (17%)
  matrix products  44.9 us (12%)
  local copies, waits for them, and re-layouts  21.5 us (6%)
  between operations  14.7 us (4%)
  other arithmetic  14.4 us (4%)
  starting transfers between devices  6.18 us (2%)
    unnamed x4, waiting for transfers between devices  109 us
    reduce_scatter x1, waiting for transfers between devices, on_device(): lax.psum_scatter(spread(bands, docs, uppers, False), Q_AXES, scatter_dime...  62.1 us
    unnamed x1, blocking collectives  33.5 us
    all_gather x1, waiting for transfers between devices, on_device(): docs = lax.all_gather(documents, D_AXES, axis=0, tiled=True)  30.7 us
    all_gather x1, blocking collectives, on_device(): parts = lax.all_gather(row_peaks + jnp.log(masses), Q_AXES, axis=0)  28.6 us
    dot_general x9, matrix products, contract(): lax.dot_general(first_op, second_op, (((1,), (1,)), ((), ())), preferred_...  18.1 us
    dot_general x9, matrix products, spread(): lax.dot_general(bands[nested], block_part, (((0,), (0,)), ((), ())), pref...  15.9 us
    unnamed x58, local copies, waits for them, and re-layouts  13 us
  transfers between devices with their start and end apart: 4, of which 3 were waited for; matrix products, arithmetic and copies ran while one was open for 8% of the time, Pallas kernels for 0%

profile of v1, /device:TPU:0, one launch (start us, length us, event | category | flops | bytes accessed | tf_op | source)
XLA Modules:
  0.0 365.7 jit_solution(12937167340569117422)
XLA Ops:
  7.9 2.5 stack.71
  10.4 6.1 %all-to-all-start = ((bf16[8,64,2048]{2,1,0:T(8,128)(2,1)}), bf16[8,64,2048]{2,1,0:T(8,128)(2,1)S(1)}, u32[]{:S(2)}, u32[]{:S(2)}) async-start(bf16[8,64,2048]{2,1,0:T(8,128)(2,1)} %stack.71), calls=%async_computation | async-start | bytes 4194304 | tf_op jit(solution)/shard_map/all_to_all | solution.py:76
  18.1 33.5 %all-reduce = s32[512]{0:T(512)S(1)} all-reduce(s32[512]{0:T(512)S(1)} %dynamic-update-slice), channel_id=1, replica_groups=mesh['dp_0'=4,'dp_1'=2,'dp_2'=4,'dp_3'=2,'rep'=2] {'dp_0','dp_1'}, use_global_device_ids=true, to_apply=%add | all-reduce | flops 512 | bytes 4096
  51.6 30.7 %all-gather.2.cloned.1.call-done = bf16[1024,2048]{1,0:T(8,128)(2,1)} async-done(((bf16[64,2048]{1,0:T(8,128)(2,1)}), bf16[1024,2048]{1,0:T(8,128)(2,1)}) %all-gather.2.cloned.1.call-update) | async-done | bytes 4194320 | tf_op jit(solution)/shard_map/all_gather | solution.py:79
  82.2 1.5 multiply_reduce_fusion.7
  84.3 1.6 multiply_reduce_fusion.6
  86.5 1.8 multiply_reduce_fusion.5
  88.8 1.8 multiply_reduce_fusion.4
  91.2 1.8 multiply_reduce_fusion.3
  93.5 1.7 multiply_reduce_fusion.2
  95.8 1.9 multiply_reduce_fusion.1
  98.2 2.4 multiply_reduce_fusion
  101.2 3.5 fusion.92
  104.7 1.4 copy-done.17
  106.7 28.6 %all_gather.11 = f32[8,9,512]{2,1,0:T(8,128)S(1)} all-gather(f32[1,9,512]{2,1,0:T(8,128)S(1)} %log_add_fusion.1), channel_id=1, replica_groups=mesh['dp_0'=4,'dp_1'=2,'dp_2'=4,'dp_3'=2,'rep'=2] {'dp_0','dp_1'}, dimensions={0}, use_global_device_ids=true | all-gather | bytes 165888 | tf_op jit(solution)/shard_map/all_gather | solution.py:93
  135.5 9.6 %fusion.17 = (bf16[512,1024]{1,0:T(8,128)(2,1)S(1)}, bf16[512,1024]{1,0:T(8,128)(2,1)S(1)}, bf16[512,1024]{1,0:T(8,128)(2,1)S(1)}, bf16[512,1024]{1,0:T(8,128)(2...) fusion(f32[512,1024]{1,0:T(8,128)S(1)} %get-tuple-element.24, ...), kind=kLoop, calls=%fused_computation.27 | loop fusion | flops 27787264 | bytes 27287552 | tf_op jit(solution)/shard_map/convert_element_type | solution.py:44
  145.2 1.4 fusion.18
  147.1 1.2 fusion.48
  148.3 1.2 fusion.45
  150.8 1.2 fusion.39
  153.2 1.2 fusion.33
  154.4 1.7 fusion.27
  156.1 5.9 %concatenate.20 = f32[512,2048]{1,0:T(8,128)} concatenate(f32[512,8]{1,0:T(8,128)S(1)} %fusion.66, f32[512,8]{1,0:T(8,128)} %fusion.48, f32[512,16]{1,0:T(8,128)} %fusion.45, f32[512,32]{1,0:T(8,128)} %fusion.42, f32[512,64]{1,0:T(8,128)} %fusion.39, f32[512,128]{1,0:T(8,128)} %fusion.36, f32[512,256]{1,0:T(8,128)} %fusion.33, f32[512,512]{1,0:T(8,128)} %fusion.27, ...), dimensions={1} | concatenate | bytes 8388608 | tf_op jit(solution)/shard_map/concatenate | solution.py:64
  162.1 1.5 copy-done.8
  163.6 2.2 convolution_dynamic-update-slice_fusion.8
  165.8 2.3 convolution_dynamic-update-slice_fusion.7
  172.4 1.5 convolution_dynamic-update-slice_fusion.2
  174.0 2.0 convolution_dynamic-update-slice_fusion.1
  176.0 3.5 convolution_dynamic-update-slice_fusion
  179.5 9.1 %copy.31 = f32[1024,2048]{1,0:T(8,128)} copy(f32[1024,2048]{0,1:T(8,128)} %convolution_dynamic-update-slice_fusion) | data formatting | bytes 16777216
  188.7 62.1 %reduce-scatter.5.cloned.1.call-done = f32[64,2048]{1,0:T(8,128)} async-done(((f32[512,2048]{1,0:T(8,128)}), f32[64,2048]{1,0:T(8,128)}) %reduce-scatter.5.cloned.1.call-update) | async-done | bytes 524304 | tf_op jit(solution)/shard_map/reduce_scatter | solution.py:102
  250.8 108.4 %reduce-scatter.7.cloned.1.call-done = f32[64,2048]{1,0:T(8,128)} async-done(((f32[1024,2048]{1,0:T(8,128)}), f32[64,2048]{1,0:T(8,128)}) %reduce-scatter.7.cloned.1.call-update) | async-done | bytes 524304
  (86 shorter events, 13.8 us)
Async XLA Ops:
  7.2 75.1 %all-gather.2.cloned.1.call-start = ((), (), s32[]{:S(2)}) async-start(), calls=%async_computation.3 | async-start | bytes 4456448 | tf_op jit(solution)/shard_map/all_gather | solution.py:79
  10.4 6.1 %copy-start.26 = (u32[128]{0:T(128)S(1)}, u32[128]{0:T(128)}, u32[]{:S(2)}) copy-start(u32[128]{0:T(128)} %constant.45) | copy-start | bytes 1540
  10.4 7.4 %copy-start.25 = (s32[64]{0:T(128)S(1)}, s32[64]{0:T(128)}, u32[]{:S(2)}) copy-start(s32[64]{0:T(128)} %param.5) | copy-start | bytes 772
  10.4 41.1 %all-to-all-start = ((bf16[8,64,2048]{2,1,0:T(8,128)(2,1)}), bf16[8,64,2048]{2,1,0:T(8,128)(2,1)S(1)}, u32[]{:S(2)}, u32[]{:S(2)}) async-start(bf16[8,64,2048]{2,1,0:T(8,128)(2,1)} %stack.71), calls=%async_computation | async-start | bytes 4194304 | tf_op jit(solution)/shard_map/all_to_all | solution.py:76
  16.5 234.3 %reduce-scatter.5.cloned.1.call-start = ((), (), s32[]{:S(2)}) async-start(), calls=%async_computation.4 | async-start | bytes 4718592 | tf_op jit(solution)/shard_map/reduce_scatter | solution.py:102
  51.6 30.7 %copy-start.7 = (bf16[8,64,2048]{2,1,0:T(8,128)(2,1)}, bf16[8,64,2048]{2,1,0:T(8,128)(2,1)S(1)}, u32[]{:S(2)}) copy-start(bf16[8,64,2048]{2,1,0:T(8,128)(2,1)S(1)} %all-to-all-done) | copy-start | bytes 6291460
  85.9 2.4 copy-start
  88.3 2.4 copy-start.1
  90.7 2.3 copy-start.2
  93.0 2.3 copy-start.3
  95.3 2.4 copy-start.4
  97.7 3.0 copy-start.5
  100.6 4.0 %copy-start.6 = (f32[512,1024]{1,0:T(8,128)}, f32[512,1024]{1,0:T(8,128)S(1)}, u32[]{:S(2)}) copy-start(f32[512,1024]{1,0:T(8,128)S(1)} %get-tuple-element.38) | copy-start | bytes 6291460
  104.7 1.4 copy-start.17
  135.5 9.7 %copy-start.18 = (f32[512,1024]{1,0:T(8,128)S(1)}, f32[512,1024]{1,0:T(8,128)}, u32[]{:S(2)}) copy-start(f32[512,1024]{1,0:T(8,128)} %copy-done.17) | copy-start | bytes 6291460
  135.5 9.7 %copy-start.20 = (bf16[1024,2048]{1,0:T(8,128)(2,1)S(1)}, bf16[1024,2048]{1,0:T(8,128)(2,1)}, u32[]{:S(2)}) copy-start(bf16[1024,2048]{1,0:T(8,128)(2,1)} %all-gather.2.cloned.1.call-done) | copy-start | bytes 12582916
  145.2 1.5 copy-start.16
  145.2 1.9 copy-start.15
  145.2 3.2 copy-start.13
  145.2 5.6 %copy-start.11 = (bf16[512,1024]{1,0:T(8,128)(2,1)}, bf16[512,1024]{1,0:T(8,128)(2,1)S(1)}, u32[]{:S(2)}) copy-start(bf16[512,1024]{1,0:T(8,128)(2,1)S(1)} %get-tuple-element.10) | copy-start | bytes 3145732
  145.2 6.8 %copy-start.9 = (bf16[512,1024]{1,0:T(8,128)(2,1)}, bf16[512,1024]{1,0:T(8,128)(2,1)S(1)}, u32[]{:S(2)}) copy-start(bf16[512,1024]{1,0:T(8,128)(2,1)S(1)} %get-tuple-element.11) | copy-start | bytes 3145732
  145.2 7.9 %copy-start.23 = (bf16[512,1024]{1,0:T(8,128)(2,1)}, bf16[512,1024]{1,0:T(8,128)(2,1)S(1)}, u32[]{:S(2)}) copy-start(bf16[512,1024]{1,0:T(8,128)(2,1)S(1)} %get-tuple-element.12) | copy-start | bytes 3145732
  145.2 9.2 %copy-start.21 = (bf16[512,1024]{1,0:T(8,128)(2,1)}, bf16[512,1024]{1,0:T(8,128)(2,1)S(1)}, u32[]{:S(2)}) copy-start(bf16[512,1024]{1,0:T(8,128)(2,1)S(1)} %get-tuple-element.13) | copy-start | bytes 3145732
  162.0 1.6 copy-start.8
  162.1 197.1 %reduce-scatter.7.cloned.1.call-start = ((), (), s32[]{:S(2)}) async-start(), calls=%async_computation.5 | async-start | bytes 8912896
  163.6 4.5 %copy-start.14 = (bf16[512,1024]{1,0:T(8,128)(2,1)S(1)}, bf16[512,1024]{1,0:T(8,128)(2,1)}, u32[]{:S(2)}) copy-start(bf16[512,1024]{1,0:T(8,128)(2,1)} %copy-done.13) | copy-start | bytes 3145732
  165.8 4.3 %copy-start.12 = (bf16[512,1024]{1,0:T(8,128)(2,1)S(1)}, bf16[512,1024]{1,0:T(8,128)(2,1)}, u32[]{:S(2)}) copy-start(bf16[512,1024]{1,0:T(8,128)(2,1)} %copy-done.11) | copy-start | bytes 3145732
  168.1 3.1 copy-start.10
  169.1 3.3 copy-start.24
  171.2 2.7 copy-start.22
  173.9 2.0 copy-start.19
Sparse Core Ops, SparseCore 0:
  10.4 71.7 all-gather.1
  162.2 88.5 reduce-scatter.4
  255.7 103.4 reduce-scatter.6
